TPU v7x, 512 devices: a whole 4x4x16 slice. The times are simulated.
512 devices in a mesh: cuts: 32 (over x, y, core), tr: 16 (over z).
Axes of the slice: x: 4, y: 4, z: 16, core: 2. Of those that a mesh axis runs over, the one named last changes fastest.
Arguments:
- cells: int32 [2, 32, 2, 1024], P(None, 'cuts'), may hold values from 1 to 509
- offsets: float32 [2, 32, 2, 1024], P(None, 'cuts'), may hold values from 0 to 1
- charges: float32 [2, 32, 1024], P(None, 'cuts'), may hold values from 0.5 to 2
- momenta: float32 [2, 32, 2, 1024], P(None, 'cuts', None, 'tr'), may hold values from -6 to 6
- green: float32 [1024, 1024], replicated, may hold values from -0.1875 to 0.1875
Outputs:
- momenta_out: float32 [2, 32, 2, 1024], P(None, 'cuts', None, 'tr')
Inputs may be any that keep to these rules, and one draw needn't show every extreme that they name: `cells`: every cell index lies in 1 .. 509.
All inputs are finite; a program needn't handle non-finite values.
Results may differ from a plain program's by a relative error of at most 0.017.
Values may be sent and summed in bfloat16 or wider, within the bound.
A program may use at most 64 MiB of HBM per device.

v0:
```python
import math
import jax
import jax.numpy as jnp
from jax import lax
from jax.sharding import PartitionSpec as P

SECTIONS = 4
drift_step = 0.5


def padded(cells, sides, width):
    for axis, dim in sides:
        count = lax.axis_size(axis)
        ends = count - 1
        head = lax.slice_in_dim(cells, 0, width, axis=dim)
        tail = lax.slice_in_dim(cells, cells.shape[dim] - width, cells.shape[dim], axis=dim)
        cells = jnp.concatenate(
            [
                lax.ppermute(tail, axis, [(i, (i + 1) % count) for i in range(ends)]),
                cells,
                lax.ppermute(head, axis, [((i + 1) % count, i) for i in range(ends)]),
            ],
            axis=dim,
        )
    return cells


def shifted(value, axis, steps):
    count = lax.axis_size(axis)
    pairs = [(source, (source + steps) % count) for source in range(count)]
    return lax.ppermute(value, axis, pairs)


def split_up(x, dim, count):
    shape = x.shape
    tiles = x.reshape(*shape[:dim], count, shape[dim] // count, *shape[dim + 1 :])
    return jnp.moveaxis(tiles, dim, 0)


def sent_and_summed(x, axis, dim):
    count = lax.axis_size(axis)
    tiles = lax.all_to_all(split_up(x, dim, count), axis, 0, 0, tiled=True)
    return jnp.sum(tiles, axis=0)


def in_order(tiles, dim):
    shape = list(tiles.shape[1:])
    shape[dim] *= tiles.shape[0]
    return jnp.moveaxis(tiles, 0, dim).reshape(shape)


def copy_for_each(x, axis):
    count = lax.axis_size(axis)
    return lax.all_to_all(jnp.broadcast_to(x[None], (count, *x.shape)), axis, 0, 0, tiled=True)


def gather_directly(x, axis, dim):
    return in_order(copy_for_each(x, axis), dim)


def phase_angles(frequency, position, period):
    return 2.0 * math.pi / period * (frequency * position % period).astype(jnp.float32)


def column_table(inputs, with_imag, begin_col, col_count, piece_width, period):
    columns = begin_col + lax.iota(jnp.int32, col_count)
    halves = columns // piece_width % 2
    frequency = columns // (2 * piece_width) * piece_width + columns % piece_width
    position = lax.iota(jnp.int32, inputs)[:, None]
    theta = phase_angles(frequency[None, :], position, period)
    cosine = jnp.cos(theta)
    sine = jnp.sin(theta)
    table = jnp.where(halves[None, :] == 0, cosine, -sine)
    if with_imag:
        lower = jnp.where(halves[None, :] == 0, sine, cosine)
        table = jnp.concatenate([table, lower], axis=0)
    return table.astype(jnp.bfloat16)


def row_table(inputs, period):
    theta = phase_angles(
        lax.iota(jnp.int32, period)[:, None], lax.iota(jnp.int32, inputs)[None, :], period
    )
    return jnp.concatenate([jnp.cos(theta), jnp.sin(theta)], axis=0).astype(jnp.bfloat16)


def forward_rows(table, spectrum, piece_width):
    both_parts = jnp.dot(table, spectrum, preferred_element_type=jnp.float32)
    period = table.shape[0] // 2
    cosine_part = both_parts[:period]
    sine_part = both_parts[period:]
    real_part = cosine_part[:, :piece_width] + sine_part[:, piece_width:]
    imag_part = cosine_part[:, piece_width:] - sine_part[:, :piece_width]
    return (real_part, imag_part)


def hat_weights(cells_along, fraction, first_node, node_count):
    nodes = first_node + lax.iota(jnp.int32, node_count)[None, :]
    lower = jnp.where(cells_along[:, None] == nodes, 1.0 - fraction[:, None], 0.0)
    upper = jnp.where(cells_along[:, None] + 1 == nodes, fraction[:, None], 0.0)
    return lower + upper


def deposit(cells, offsets, charges, first_node, node_rows, node_cols):
    particles = cells.shape[1]
    block_size = math.gcd(particles, 512)
    grid_sum = jnp.zeros((node_rows, node_cols), jnp.float32)
    for number in range(particles // block_size):
        begin_at = number * block_size
        finish_at = begin_at + block_size
        weight_rows = hat_weights(
            cells[0, begin_at:finish_at], offsets[0, begin_at:finish_at], first_node, node_rows
        )
        weight_cols = hat_weights(
            cells[1, begin_at:finish_at], offsets[1, begin_at:finish_at], 0, node_cols
        )
        weight_cols = charges[begin_at:finish_at][:, None] * weight_cols
        grid_sum = grid_sum + lax.dot_general(
            weight_rows.astype(jnp.bfloat16),
            weight_cols.astype(jnp.bfloat16),
            (((0,), (0,)), ((), ())),
            preferred_element_type=jnp.float32,
        )
    return grid_sum.astype(jnp.bfloat16)


def drift(cells, offsets, moment, extent):
    place = cells.astype(jnp.float32) + offsets + drift_step * moment
    place = jnp.clip(place, 1.0, extent - 2.0 - 1.0 / 64.0)
    whole = jnp.floor(place)
    return (whole.astype(jnp.int32), place - whole)


def potentials(pair_grid, pair_columns, own_columns, pair_rows, kernel_re, kernel_im, piece_width):
    spectrum = jnp.dot(pair_grid, own_columns, preferred_element_type=jnp.float32).astype(
        jnp.bfloat16
    )
    forward_re, forward_im = forward_rows(pair_rows, spectrum, piece_width)
    scaled = jnp.concatenate(
        [
            forward_re * kernel_re - forward_im * kernel_im,
            forward_re * kernel_im + forward_im * kernel_re,
        ],
        axis=1,
    ).astype(jnp.bfloat16)
    period = pair_rows.shape[0] // 2
    extent = pair_rows.shape[1]
    halves = lax.dot_general(
        pair_rows.reshape(2, period, extent),
        scaled,
        (((1,), (0,)), ((), ())),
        preferred_element_type=jnp.float32,
    )
    cosine_part = halves[0]
    sine_part = halves[1]
    inverse = jnp.concatenate(
        [
            cosine_part[:, :piece_width] - sine_part[:, piece_width:],
            cosine_part[:, piece_width:] + sine_part[:, :piece_width],
        ],
        axis=1,
    ).astype(jnp.bfloat16)
    inverse = lax.all_to_all(inverse, "tr", split_axis=0, concat_axis=1, tiled=True)
    potential = lax.dot_general(
        inverse, pair_columns, (((1,), (1,)), ((), ())), preferred_element_type=jnp.float32
    ) * (1.0 / (period * period))
    return potential.reshape(potential.shape[0], 2, extent)


def field_grids(potential):
    widened = padded(potential.astype(jnp.bfloat16), (("tr", 0),), 1).astype(potential.dtype)
    along_rows = (widened[:-2] - widened[2:]) * 0.5
    sideways = jnp.pad(potential, ((0, 0), (0, 0), (1, 1)))
    along_cols = (sideways[:, :, :-2] - sideways[:, :, 2:]) * 0.5
    stacked = jnp.stack([along_rows, along_cols], axis=0)
    node_rows = potential.shape[0]
    return (
        jnp.transpose(stacked, (2, 0, 1, 3))
        .reshape(2, 2 * node_rows, potential.shape[2])
        .astype(jnp.bfloat16)
    )


def kick_terms(cells, offsets, fields, first_node, node_rows, row_count):
    node_cols = fields.shape[2]
    block_size = math.gcd(row_count, 256)

    def one_block(number):
        begin_at = number * block_size
        columns = []
        for beam_index in range(2):
            row_cells = lax.dynamic_slice_in_dim(cells[beam_index, 0], begin_at, block_size)
            col_cells = lax.dynamic_slice_in_dim(cells[beam_index, 1], begin_at, block_size)
            row_frac = lax.dynamic_slice_in_dim(offsets[beam_index, 0], begin_at, block_size)
            col_frac = lax.dynamic_slice_in_dim(offsets[beam_index, 1], begin_at, block_size)
            weight_rows = hat_weights(row_cells, row_frac, first_node, node_rows).astype(
                jnp.bfloat16
            )
            weight_cols = hat_weights(col_cells, col_frac, 0, node_cols).astype(jnp.bfloat16)
            projected = lax.dot_general(
                weight_cols,
                fields[1 - beam_index],
                (((1,), (1,)), ((), ())),
                preferred_element_type=jnp.float32,
            )
            projected = projected.reshape(block_size, 2, node_rows)
            columns.append(jnp.sum(projected * weight_rows.astype(jnp.float32)[:, None, :], axis=2))
        return jnp.concatenate(columns, axis=1)

    blocks = lax.map(one_block, jnp.arange(row_count // block_size, dtype=jnp.int32))
    return blocks.reshape(row_count, 4)


def per_device(cells, offsets, charges, momenta, green):
    shards = lax.axis_size("tr")
    shard_index = lax.axis_index("tr")
    period = green.shape[0]
    extent = period // 2
    node_rows = extent // shards
    piece_width = period // shards
    first_node = shard_index * node_rows
    kernel_columns = column_table(
        period, False, shard_index * 2 * piece_width, 2 * piece_width, piece_width, period
    )
    kernel_cols = jnp.dot(
        green.astype(jnp.bfloat16), kernel_columns, preferred_element_type=jnp.float32
    ).astype(jnp.bfloat16)
    kernel_re, kernel_im = forward_rows(row_table(period, period), kernel_cols, piece_width)
    pair_columns = column_table(extent, True, 0, 2 * period, piece_width, period)
    pair_rows = row_table(extent, period)
    own_columns = column_table(
        extent, True, shard_index * 2 * piece_width, 2 * piece_width, piece_width, period
    )
    deposit_first = 0
    local_cells = cells[:, 0]
    local_offsets = offsets[:, 0]
    local_charges = charges[:, 0]
    moment = momenta
    particle_rows = momenta.shape[-1]
    for section_index in range(SECTIONS):
        charge_grids = [
            deposit(
                local_cells[beam_index],
                local_offsets[beam_index],
                local_charges[beam_index],
                deposit_first,
                extent,
                extent,
            )
            for beam_index in range(2)
        ]
        if section_index > 0:
            charge_grids = [
                shifted(charge_grids[0], "cuts", 2 * section_index),
                shifted(charge_grids[1], "cuts", -2 * section_index),
            ]
        pair_grid = jnp.concatenate(charge_grids, axis=1)
        potential = potentials(
            pair_grid, pair_columns, own_columns, pair_rows, kernel_re, kernel_im, piece_width
        )
        fields = field_grids(potential)
        kick_sums = sent_and_summed(
            kick_terms(
                local_cells,
                local_offsets,
                fields,
                first_node,
                node_rows,
                particle_rows * lax.axis_size("tr"),
            ),
            "tr",
            0,
        )
        moment = moment + jnp.transpose(kick_sums).reshape(moment.shape)
        if section_index + 1 < SECTIONS:
            whole_moment = gather_directly(moment, "tr", 3)
            local_cells, local_offsets = drift(
                local_cells, local_offsets, whole_moment[:, 0], extent
            )
    return moment


def solution(mesh):
    return jax.shard_map(
        per_device,
        mesh=mesh,
        in_specs=(
            P(None, "cuts", None, None),
            P(None, "cuts", None, None),
            P(None, "cuts", None),
            P(None, "cuts", None, "tr"),
            P(),
        ),
        out_specs=P(None, "cuts", None, "tr"),
        check_vma=False,
    )
```

profile of v0, /device:TPU:6, one launch (start us, length us, event | category | flops | bytes accessed | tf_op | source)
XLA Modules:
  0.0 439.0 jit_solution(6951870104126059463)
XLA Ops:
  0.0 8.5 %fusion.147 = (bf16[1024,512]{1,0:T(8,128)(2,1)S(1)}, bf16[1024,512]{1,0:T(8,128)(2,1)S(1)}) fusion(), kind=kLoop, calls=%fused_computation.362 | loop fusion | flops 8388608 | bytes 2097152 | tf_op jit(solution)/shard_map/sin | solution.py:84
  8.6 17.7 %sine_convert_fusion = (bf16[1024,1024]{1,0:T(8,128)(2,1)}, bf16[1024,1024]{1,0:T(8,128)(2,1)}) fusion(), kind=kLoop, calls=%fused_computation.206 | loop fusion | flops 16777216 | bytes 4194304 | tf_op jit(solution)/shard_map/convert.43
  28.2 8.5 %fusion.86 = f32[2048,128]{0,1:T(8,128)} fusion(bf16[1024,1024]{1,0:T(8,128)(2,1)} %get-tuple-element.438, bf16[1024,1024]{1,0:T(8,128)(2,1)} %get-tuple-element.439, f32[1024,1024]{1,0:T(8,128)} %param.17, s32[128]{0:T(128)S(1)} %fusion.412, pred[128]{0:T(512)(128)(4,1)S(1)} %fusion.413), kind=kOutput, calls=%fused_computation.197 | convolution fusion | flops 817102848 | bytes 9437824 | tf_op jit(solution)/shard_map/dot_general | solution.py:88
  49.1 15.7 %all-to-all-start = ((bf16[16,32,128]{2,1,0:T(8,128)(2,1)}), bf16[16,32,128]{2,1,0:T(8,128)(2,1)S(1)}, u32[]{:S(2)}, u32[]{:S(2)}) async-start(bf16[16,32,128]{2,1,0:T(8,128)(2,1)} %pad_maximum_fusion.2), calls=%async_computation | async-start | bytes 262144 | tf_op jit(solution)/shard_map/all_to_all | solution.py:163
  64.9 18.5 %select_convert_fusion.1 = (bf16[512,2048]{1,0:T(8,128)(2,1)}, bf16[512,2048]{1,0:T(8,128)(2,1)}) fusion(s32[2048]{0:T(1024)S(1)} %fusion.409, pred[2048]{0:T(1024)(128)(4,1)S(1)} %fusion.406), kind=kLoop, calls=%fused_computation.203 | loop fusion | flops 19922944 | bytes 4204544 | tf_op jit(solution)/shard_map/convert.34
  97.3 9.5 %while.40 = (s32[]{:T(128)}, f32[4,256,4]{1,0,2:T(4,128)S(1)}, s32[2,2,1024]{2,1,0:T(2,128)S(1)}, s32[4]{0:T(128)S(1)}, f32[2,2,1024]{2,1,0:T(2,128)S(1)}, /*ind...) while((s32[]{:T(128)}, f32[4,256,4]{1,0,2:T(4,128)S(1)}, ...), condition=%wide.region_3.4_spmd, body=%wide.region_0.3_spmd.sunk | while | flops 35309604 | bytes 668095 | solution.py:210
  107.0 24.2 %all_to_all.99 = f32[16,1,256]{2,1,0:T(1,128)S(1)} all-to-all(f32[16,1,256]{2,1,0:T(1,128)S(1)} %reshape.1728), channel_id=1, replica_groups=mesh['cuts'=32,'tr'=16] {'tr'}, dimensions={0} | all-to-all | bytes 32768 | tf_op jit(solution)/shard_map/all_to_all | solution.py:42
  132.7 15.0 %all_to_all.100 = f32[16,1,256]{2,1,0:T(1,128)S(1)} all-to-all(f32[16,1,256]{2,1,0:T(1,128)S(1)} %reshape.1730), channel_id=1, replica_groups=mesh['cuts'=32,'tr'=16] {'tr'}, dimensions={0} | all-to-all | bytes 32768 | tf_op jit(solution)/shard_map/all_to_all | solution.py:54
  157.1 4.6 %collective-permute-start.3 = (bf16[512,512]{1,0:T(8,128)(2,1)S(1)}, bf16[512,512]{1,0:T(8,128)(2,1)}, u32[]{:S(2)}, u32[]{:S(2)}) collective-permute-start(bf16[512,512]{1,0:T(8,128)(2,1)S(1)} %fusion.109), channel_id=1, source_target_pairs={{0,480},{16,496},{32,0},{48,16},{64,32},{80,48},{96,64},{112,80},{... | collective-permute-start | bytes 1572872 | tf_op jit(solution)/shard_map/ppermute | solution.py:31
  174.5 15.9 %all_to_all.101 = bf16[16,32,128]{2,1,0:T(8,128)(2,1)S(1)} all-to-all(bf16[16,32,128]{2,1,0:T(8,128)(2,1)S(1)} %pad_maximum_fusion.3), channel_id=1, replica_groups=mesh['cuts'=32,'tr'=16] {'tr'}, dimensions={0} | all-to-all | bytes 262144 | tf_op jit(solution)/shard_map/all_to_all | solution.py:163
  203.4 9.6 %while.41 = (s32[]{:T(128)}, f32[4,256,4]{1,0,2:T(4,128)S(1)}, s32[2,2,1024]{2,1,0:T(2,128)S(1)}, s32[4]{0:T(128)S(1)}, f32[2,2,1024]{2,1,0:T(2,128)S(1)}, /*ind...) while((s32[]{:T(128)}, f32[4,256,4]{1,0,2:T(4,128)S(1)}, ...), condition=%wide.region_8.9_spmd, body=%wide.region_5.8_spmd.sunk | while | flops 35309604 | bytes 668095 | solution.py:210
  213.2 18.6 %all_to_all.102 = f32[16,1,256]{2,1,0:T(1,128)S(1)} all-to-all(f32[16,1,256]{2,1,0:T(1,128)S(1)} %reshape.1732), channel_id=1, replica_groups=mesh['cuts'=32,'tr'=16] {'tr'}, dimensions={0} | all-to-all | bytes 32768 | tf_op jit(solution)/shard_map/all_to_all | solution.py:42
  232.6 15.0 %all_to_all.103 = f32[16,1,256]{2,1,0:T(1,128)S(1)} all-to-all(f32[16,1,256]{2,1,0:T(1,128)S(1)} %reshape.1734), channel_id=1, replica_groups=mesh['cuts'=32,'tr'=16] {'tr'}, dimensions={0} | all-to-all | bytes 32768 | tf_op jit(solution)/shard_map/all_to_all | solution.py:54
  251.0 4.8 %collective-permute-start.6 = (bf16[512,512]{1,0:T(8,128)(2,1)S(1)}, bf16[512,512]{1,0:T(8,128)(2,1)}, u32[]{:S(2)}, u32[]{:S(2)}) collective-permute-start(bf16[512,512]{1,0:T(8,128)(2,1)S(1)} %fusion.110), channel_id=1, source_target_pairs={{0,64},{16,80},{32,96},{48,112},{64,128},{80,144},{96,160},{112,17... | collective-permute-start | bytes 1572872 | tf_op jit(solution)/shard_map/ppermute | solution.py:31
  264.6 6.4 %collective-permute-done.7 = bf16[512,512]{1,0:T(8,128)(2,1)} collective-permute-done((bf16[512,512]{1,0:T(8,128)(2,1)S(1)}, bf16[512,512]{1,0:T(8,128)(2,1)}, u32[]{:S(2)}, u32[]{:S(2)}) %collective-permute-start.7) | collective-permute-done | bytes 524320 | tf_op jit(solution)/shard_map/ppermute | solution.py:31
  277.0 15.7 %all_to_all.104 = bf16[16,32,128]{2,1,0:T(8,128)(2,1)S(1)} all-to-all(bf16[16,32,128]{2,1,0:T(8,128)(2,1)S(1)} %pad_maximum_fusion.4), channel_id=1, replica_groups=mesh['cuts'=32,'tr'=16] {'tr'}, dimensions={0} | all-to-all | bytes 262144 | tf_op jit(solution)/shard_map/all_to_all | solution.py:163
  305.7 9.8 %while.42 = (s32[]{:T(128)}, f32[4,256,4]{1,0,2:T(4,128)S(1)}, s32[2,2,1024]{2,1,0:T(2,128)S(1)}, s32[4]{0:T(128)S(1)}, f32[2,2,1024]{2,1,0:T(2,128)S(1)}, /*ind...) while((s32[]{:T(128)}, f32[4,256,4]{1,0,2:T(4,128)S(1)}, ...), condition=%wide.region_13.14_spmd, body=%wide.region_10.13_spmd.sunk | while | flops 35309604 | bytes 668095 | solution.py:210
  315.6 18.7 %all_to_all.105 = f32[16,1,256]{2,1,0:T(1,128)S(1)} all-to-all(f32[16,1,256]{2,1,0:T(1,128)S(1)} %reshape.1736), channel_id=1, replica_groups=mesh['cuts'=32,'tr'=16] {'tr'}, dimensions={0} | all-to-all | bytes 32768 | tf_op jit(solution)/shard_map/all_to_all | solution.py:42
  335.2 15.0 %all_to_all.106 = f32[16,1,256]{2,1,0:T(1,128)S(1)} all-to-all(f32[16,1,256]{2,1,0:T(1,128)S(1)} %reshape.1738), channel_id=1, replica_groups=mesh['cuts'=32,'tr'=16] {'tr'}, dimensions={0} | all-to-all | bytes 32768 | tf_op jit(solution)/shard_map/all_to_all | solution.py:54
  353.6 6.0 %collective-permute-start.10 = (bf16[512,512]{1,0:T(8,128)(2,1)S(1)}, bf16[512,512]{1,0:T(8,128)(2,1)S(1)}, u32[]{:S(2)}, u32[]{:S(2)}) collective-permute-start(bf16[512,512]{1,0:T(8,128)(2,1)S(1)} %fusion.112), channel_id=1, source_target_pairs={{0,96},{16,112},{32,128},{48,144},{64,160},{80,176},{96,192},{112,... | collective-permute-start | bytes 1572872 | tf_op jit(solution)/shard_map/ppermute | solution.py:31
  366.3 8.2 %collective-permute-done.11 = bf16[512,512]{1,0:T(8,128)(2,1)} collective-permute-done((bf16[512,512]{1,0:T(8,128)(2,1)S(1)}, bf16[512,512]{1,0:T(8,128)(2,1)}, u32[]{:S(2)}, u32[]{:S(2)}) %collective-permute-start.11) | collective-permute-done | bytes 524320 | tf_op jit(solution)/shard_map/ppermute | solution.py:31
  380.4 15.8 %all_to_all.107 = bf16[16,32,128]{2,1,0:T(8,128)(2,1)S(1)} all-to-all(bf16[16,32,128]{2,1,0:T(8,128)(2,1)S(1)} %pad_maximum_fusion.5), channel_id=1, replica_groups=mesh['cuts'=32,'tr'=16] {'tr'}, dimensions={0} | all-to-all | bytes 262144 | tf_op jit(solution)/shard_map/all_to_all | solution.py:163
  408.5 10.0 %while.43 = (s32[]{:T(128)}, f32[4,256,4]{1,0,2:T(4,128)S(1)}, s32[2,2,1024]{2,1,0:T(2,128)S(1)}, s32[4]{0:T(128)S(1)}, f32[2,2,1024]{2,1,0:T(2,128)S(1)}, /*ind...) while((s32[]{:T(128)}, f32[4,256,4]{1,0,2:T(4,128)S(1)}, ...), condition=%wide.region_18.19_spmd, body=%wide.region_15.18_spmd.sunk | while | flops 35309604 | bytes 668095 | solution.py:210
  418.8 18.7 %all_to_all.108 = f32[16,1,256]{2,1,0:T(1,128)S(1)} all-to-all(f32[16,1,256]{2,1,0:T(1,128)S(1)} %reshape.1740), channel_id=1, replica_groups=mesh['cuts'=32,'tr'=16] {'tr'}, dimensions={0} | all-to-all | bytes 32768 | tf_op jit(solution)/shard_map/all_to_all | solution.py:42
  (666 shorter events, 152.2 us)
Async XLA Ops:
  8.5 17.8 %copy-start.5 = (s32[2,1,2,1024]{3,2,1,0:T(2,128)S(1)}, s32[2,1,2,1024]{3,2,1,0:T(2,128)}, u32[]{:S(2)}) copy-start(s32[2,1,2,1024]{3,2,1,0:T(2,128)} %param.13) | copy-start | bytes 49156
  8.5 17.8 %copy-start.6 = (f32[2,1,2,1024]{3,2,1,0:T(2,128)S(1)}, f32[2,1,2,1024]{3,2,1,0:T(2,128)}, u32[]{:S(2)}) copy-start(f32[2,1,2,1024]{3,2,1,0:T(2,128)} %param.14) | copy-start | bytes 49156
  8.6 17.9 %copy-start.8 = (f32[2,1,1024]{2,1,0:T(1,128)S(1)}, f32[2,1,1024]{2,1,0:T(1,128)}, u32[]{:S(2)}) copy-start(f32[2,1,1024]{2,1,0:T(1,128)} %param.15) | copy-start | bytes 24580
  26.5 14.7 %copy-start.10 = (f32[1,1,512]{2,1,0:T(1,128)}, f32[1,1,512]{2,1,0:T(1,128)S(1)}, u32[]{:S(2)}) copy-start(f32[1,1,512]{2,1,0:T(1,128)S(1)} %get-tuple-element.416) | copy-start | bytes 6148
  28.1 15.1 %copy-start.2 = (bf16[512,128]{1,0:T(8,128)(2,1)}, bf16[512,128]{1,0:T(8,128)(2,1)S(1)}, u32[]{:S(2)}) copy-start(bf16[512,128]{1,0:T(8,128)(2,1)S(1)} %get-tuple-element.427) | copy-start | bytes 393220
  49.1 34.2 %all-to-all-start = ((bf16[16,32,128]{2,1,0:T(8,128)(2,1)}), bf16[16,32,128]{2,1,0:T(8,128)(2,1)S(1)}, u32[]{:S(2)}, u32[]{:S(2)}) async-start(bf16[16,32,128]{2,1,0:T(8,128)(2,1)} %pad_maximum_fusion.2), calls=%async_computation | async-start | bytes 262144 | tf_op jit(solution)/shard_map/all_to_all | solution.py:163
  87.5 5.2 %collective-permute-start = (bf16[1,2,512]{2,1,0:T(2,128)(2,1)S(1)}, bf16[1,2,512]{2,1,0:T(2,128)(2,1)S(1)}, u32[]{:S(2)}, u32[]{:S(2)}) collective-permute-start(bf16[1,2,512]{2,1,0:T(2,128)(2,1)S(1)} %get-tuple-element.338), channel_id=1, source_target_pairs={{0,1},{1,2},{2,3},{3,4},{4,5},{5,6},{6,7},{7,8},{8,9},{9,10},{10,1... | collective-permute-start | bytes 6152 | tf_op jit(solution)/shard_map/ppermute | solution.py:19
  91.4 5.5 %collective-permute-start.1 = (bf16[1,2,512]{2,1,0:T(2,128)(2,1)S(1)}, bf16[1,2,512]{2,1,0:T(2,128)(2,1)S(1)}, u32[]{:S(2)}, u32[]{:S(2)}) collective-permute-start(bf16[1,2,512]{2,1,0:T(2,128)(2,1)S(1)} %get-tuple-element.339), channel_id=1, source_target_pairs={{1,0},{2,1},{3,2},{4,3},{5,4},{6,5},{7,6},{8,7},{9,8},{10,9},{11,1... | collective-permute-start | bytes 6152 | tf_op jit(solution)/shard_map/ppermute | solution.py:21
  97.3 35.3 %copy-start.9 = (f32[2,1,2,64]{3,2,1,0:T(2,128)S(1)}, f32[2,1,2,64]{3,2,1,0:T(2,128)}, u32[]{:S(2)}) copy-start(f32[2,1,2,64]{3,2,1,0:T(2,128)} %param.16) | copy-start | bytes 3076
  97.3 51.4 %copy-start.17 = (f32[1,1,512]{2,1,0:T(1,128)S(1)}, f32[1,1,512]{2,1,0:T(1,128)}, u32[]{:S(2)}) copy-start(f32[1,1,512]{2,1,0:T(1,128)} %copy-done.16) | copy-start | bytes 6148
  151.1 13.3 %collective-permute-start.2 = (bf16[512,512]{1,0:T(8,128)(2,1)S(1)}, bf16[512,512]{1,0:T(8,128)(2,1)}, u32[]{:S(2)}, u32[]{:S(2)}) collective-permute-start(bf16[512,512]{1,0:T(8,128)(2,1)S(1)} %fusion.108), channel_id=1, source_target_pairs={{0,32},{16,48},{32,64},{48,80},{64,96},{80,112},{96,128},{112,144}... | collective-permute-start | bytes 1572872 | tf_op jit(solution)/shard_map/ppermute | solution.py:31
  157.1 15.2 %copy-start.1 = (f32[1024,64]{0,1:T(8,128)S(1)}, f32[1024,64]{0,1:T(8,128)}, u32[]{:S(2)}) copy-start(f32[1024,64]{0,1:T(8,128)} %copy-done) | copy-start | bytes 786436
  157.1 11.3 %collective-permute-start.3 = (bf16[512,512]{1,0:T(8,128)(2,1)S(1)}, bf16[512,512]{1,0:T(8,128)(2,1)}, u32[]{:S(2)}, u32[]{:S(2)}) collective-permute-start(bf16[512,512]{1,0:T(8,128)(2,1)S(1)} %fusion.109), channel_id=1, source_target_pairs={{0,480},{16,496},{32,0},{48,16},{64,32},{80,48},{96,64},{112,80},{... | collective-permute-start | bytes 1572872 | tf_op jit(solution)/shard_map/ppermute | solution.py:31
  194.5 4.3 collective-permute-start.4
  197.5 5.5 %collective-permute-start.5 = (bf16[1,2,512]{2,1,0:T(2,128)(2,1)S(1)}, bf16[1,2,512]{2,1,0:T(2,128)(2,1)S(1)}, u32[]{:S(2)}, u32[]{:S(2)}) collective-permute-start(bf16[1,2,512]{2,1,0:T(2,128)(2,1)S(1)} %get-tuple-element.337), channel_id=1, source_target_pairs={{1,0},{2,1},{3,2},{4,3},{5,4},{6,5},{7,6},{8,7},{9,8},{10,9},{11,1... | collective-permute-start | bytes 6152 | tf_op jit(solution)/shard_map/ppermute | solution.py:21
  251.0 13.6 %collective-permute-start.6 = (bf16[512,512]{1,0:T(8,128)(2,1)S(1)}, bf16[512,512]{1,0:T(8,128)(2,1)}, u32[]{:S(2)}, u32[]{:S(2)}) collective-permute-start(bf16[512,512]{1,0:T(8,128)(2,1)S(1)} %fusion.110), channel_id=1, source_target_pairs={{0,64},{16,80},{32,96},{48,112},{64,128},{80,144},{96,160},{112,17... | collective-permute-start | bytes 1572872 | tf_op jit(solution)/shard_map/ppermute | solution.py:31
  258.3 12.7 %collective-permute-start.7 = (bf16[512,512]{1,0:T(8,128)(2,1)S(1)}, bf16[512,512]{1,0:T(8,128)(2,1)}, u32[]{:S(2)}, u32[]{:S(2)}) collective-permute-start(bf16[512,512]{1,0:T(8,128)(2,1)S(1)} %fusion.111), channel_id=1, source_target_pairs={{0,448},{16,464},{32,480},{48,496},{64,0},{80,16},{96,32},{112,48}... | collective-permute-start | bytes 1572872 | tf_op jit(solution)/shard_map/ppermute | solution.py:31
  296.8 4.3 collective-permute-start.8
  299.8 5.5 %collective-permute-start.9 = (bf16[1,2,512]{2,1,0:T(2,128)(2,1)S(1)}, bf16[1,2,512]{2,1,0:T(2,128)(2,1)S(1)}, u32[]{:S(2)}, u32[]{:S(2)}) collective-permute-start(bf16[1,2,512]{2,1,0:T(2,128)(2,1)S(1)} %get-tuple-element.335), channel_id=1, source_target_pairs={{1,0},{2,1},{3,2},{4,3},{5,4},{6,5},{7,6},{8,7},{9,8},{10,9},{11,1... | collective-permute-start | bytes 6152 | tf_op jit(solution)/shard_map/ppermute | solution.py:21
  353.6 12.7 %collective-permute-start.10 = (bf16[512,512]{1,0:T(8,128)(2,1)S(1)}, bf16[512,512]{1,0:T(8,128)(2,1)S(1)}, u32[]{:S(2)}, u32[]{:S(2)}) collective-permute-start(bf16[512,512]{1,0:T(8,128)(2,1)S(1)} %fusion.112), channel_id=1, source_target_pairs={{0,96},{16,112},{32,128},{48,144},{64,160},{80,176},{96,192},{112,... | collective-permute-start | bytes 1572872 | tf_op jit(solution)/shard_map/ppermute | solution.py:31
  362.1 12.4 %collective-permute-start.11 = (bf16[512,512]{1,0:T(8,128)(2,1)S(1)}, bf16[512,512]{1,0:T(8,128)(2,1)}, u32[]{:S(2)}, u32[]{:S(2)}) collective-permute-start(bf16[512,512]{1,0:T(8,128)(2,1)S(1)} %fusion.113), channel_id=1, source_target_pairs={{0,416},{16,432},{32,448},{48,464},{64,480},{80,496},{96,0},{112,1... | collective-permute-start | bytes 1572872 | tf_op jit(solution)/shard_map/ppermute | solution.py:31
  379.9 16.3 %copy-start.4 = (bf16[512,2048]{1,0:T(8,128)(2,1)S(1)}, bf16[512,2048]{1,0:T(8,128)(2,1)}, u32[]{:S(2)}) copy-start(bf16[512,2048]{1,0:T(8,128)(2,1)} %get-tuple-element.356) | copy-start | bytes 6291460
  399.6 4.3 collective-permute-start.12
  402.7 5.5 %collective-permute-start.13 = (bf16[1,2,512]{2,1,0:T(2,128)(2,1)S(1)}, bf16[1,2,512]{2,1,0:T(2,128)(2,1)S(1)}, u32[]{:S(2)}, u32[]{:S(2)}) collective-permute-start(bf16[1,2,512]{2,1,0:T(2,128)(2,1)S(1)} %get-tuple-element.333), channel_id=1, source_target_pairs={{1,0},{2,1},{3,2},{4,3},{5,4},{6,5},{7,6},{8,7},{9,8},{10,9},{11,1... | collective-permute-start | bytes 6152 | tf_op jit(solution)/shard_map/ppermute | solution.py:21
  (9 other events, 68.8 us)
where the time goes:
time: 443 us; the launch traced here: 439 us
  blocking collectives  172 us (39%)
  matrix products  69.9 us (16%)
  other arithmetic  63.3 us (14%)
  starting transfers between devices  58.1 us (13%)
  waiting for transfers between devices  43.1 us (10%)
  local copies, waits for them, and re-layouts  16.7 us (4%)
  loops' own time  13.3 us (3%)
    all_to_all x4, blocking collectives, sent_and_summed(): tiles = lax.all_to_all(split_up(x, dim, count), axis, 0, 0, tiled=True)  80.1 us
    all_to_all x3, blocking collectives, potentials(): lax.all_to_all(inverse, 'tr', split_axis=0, concat_axis=1, tiled=True)  47.4 us
    all_to_all x3, blocking collectives, copy_for_each(): lax.all_to_all(jnp.broadcast_to(x[None], (count, *x.shape)), axis, 0, 0,...  44.9 us
    another operation x12, other arithmetic  43.2 us
    ppermute x6, waiting for transfers between devices, shifted(): return lax.ppermute(value, axis, pairs)  26.4 us
    ppermute x6, starting transfers between devices, shifted(): return lax.ppermute(value, axis, pairs)  24.3 us
    dot_general x5, matrix products, forward_rows(): both_parts = jnp.dot(table, spectrum, preferred_element_type=jnp.float32)  22.7 us
    dot_general x16, matrix products, deposit(): lax.dot_general(weight_rows.astype(jnp.bfloat16), weight_cols.astype(jnp....  20.4 us
  transfers between devices with their start and end apart: 15, of which 10 were waited for; matrix products, arithmetic and copies ran while one was open for 6% of the time, Pallas kernels for 0%

commit v1 on v0

--- a/solution.py
+++ b/solution.py
@@ -160,7 +160,10 @@
         ],
         axis=1,
     ).astype(jnp.bfloat16)
-    inverse = lax.all_to_all(inverse, "tr", split_axis=0, concat_axis=1, tiled=True)
+    size = lax.axis_size("tr")
+    pieces = jnp.stack(jnp.split(inverse, size, axis=0), axis=0)
+    pieces = lax.all_to_all(pieces, "tr", split_axis=0, concat_axis=0)
+    inverse = jnp.concatenate(pieces, axis=1)
     potential = lax.dot_general(
         inverse, pair_columns, (((1,), (1,)), ((), ())), preferred_element_type=jnp.float32
     ) * (1.0 / (period * period))

time: 443 us -> 463 us (1.045)
  local copies, waits for them, and re-layouts: 16.7 us -> 35.8 us
    unnamed x53 -> x131, local copies, waits for them, and re-layouts: 1.5 us -> 12.2 us
    another operation x12 -> x72, local copies, waits for them, and re-layouts: 0.97 us -> 9.13 us  [the longest x68 9.11 us: potentials(): pieces = jnp.stack(jnp.split(inverse, size, axis=0), axis=0)]
    another operation x12 -> x20, other arithmetic: 43.2 us -> 45.2 us
where the time goes in v1:
time: 463 us; the launch traced here: 459 us
  blocking collectives  173 us (37%)
  matrix products  69.9 us (15%)
  other arithmetic  64 us (14%)
  starting transfers between devices  58 us (13%)
  waiting for transfers between devices  42.9 us (9%)
  local copies, waits for them, and re-layouts  35.8 us (8%)
  loops' own time  13.4 us (3%)
    all_to_all x4, blocking collectives, sent_and_summed(): tiles = lax.all_to_all(split_up(x, dim, count), axis, 0, 0, tiled=True)  80.1 us
    all_to_all x3, blocking collectives, potentials(): pieces = lax.all_to_all(pieces, 'tr', split_axis=0, concat_axis=0)  47.5 us
    all_to_all x3, blocking collectives, copy_for_each(): lax.all_to_all(jnp.broadcast_to(x[None], (count, *x.shape)), axis, 0, 0,...  44.9 us
    another operation x12, other arithmetic  43.1 us
    ppermute x6, waiting for transfers between devices, shifted(): return lax.ppermute(value, axis, pairs)  26.4 us
    ppermute x6, starting transfers between devices, shifted(): return lax.ppermute(value, axis, pairs)  24.3 us
    dot_general x5, matrix products, forward_rows(): both_parts = jnp.dot(table, spectrum, preferred_element_type=jnp.float32)  22.7 us
    dot_general x16, matrix products, deposit(): lax.dot_general(weight_rows.astype(jnp.bfloat16), weight_cols.astype(jnp....  20.4 us
  transfers between devices with their start and end apart: 15, of which 10 were waited for; matrix products, arithmetic and copies ran while one was open for 6% of the time, Pallas kernels for 0%

profile of v1, /device:TPU:6, one launch (start us, length us, event | category | flops | bytes accessed | tf_op | source)
XLA Modules:
  0.0 458.9 jit_solution(3666324446381120338)
XLA Ops:
  0.0 8.5 %fusion.147 = (bf16[1024,512]{1,0:T(8,128)(2,1)S(1)}, bf16[1024,512]{1,0:T(8,128)(2,1)S(1)}) fusion(), kind=kLoop, calls=%fused_computation.362 | loop fusion | flops 8388608 | bytes 2097152 | tf_op jit(solution)/shard_map/sin | solution.py:84
  8.6 17.7 %sine_convert_fusion = (bf16[1024,1024]{1,0:T(8,128)(2,1)}, bf16[1024,1024]{1,0:T(8,128)(2,1)}) fusion(), kind=kLoop, calls=%fused_computation.206 | loop fusion | flops 16777216 | bytes 4194304 | tf_op jit(solution)/shard_map/convert.35
  28.1 8.5 %fusion.86 = f32[2048,128]{0,1:T(8,128)} fusion(bf16[1024,1024]{1,0:T(8,128)(2,1)} %get-tuple-element.502, bf16[1024,1024]{1,0:T(8,128)(2,1)} %get-tuple-element.503, f32[1024,1024]{1,0:T(8,128)} %param.17, s32[128]{0:T(128)S(1)} %fusion.536, pred[128]{0:T(512)(128)(4,1)S(1)} %fusion.537), kind=kOutput, calls=%fused_computation.197 | convolution fusion | flops 817102848 | bytes 9437824 | tf_op jit(solution)/shard_map/dot_general | solution.py:88
  59.3 15.4 %all-to-all-start = ((bf16[16,32,128]{2,1,0:T(8,128)(2,1)}), bf16[16,32,128]{2,1,0:T(8,128)(2,1)S(1)}, u32[]{:S(2)}, u32[]{:S(2)}) async-start(bf16[16,32,128]{2,1,0:T(8,128)(2,1)} %constant_dynamic-update-slice_fusion), calls=%async_computation | async-start | bytes 262144 | tf_op jit(solution)/shard_map/all_to_all | solution.py:165
  74.7 18.5 %select_convert_fusion.1 = (bf16[512,2048]{1,0:T(8,128)(2,1)}, bf16[512,2048]{1,0:T(8,128)(2,1)}) fusion(s32[2048]{0:T(1024)S(1)} %fusion.533, pred[2048]{0:T(1024)(128)(4,1)S(1)} %fusion.530), kind=kLoop, calls=%fused_computation.203 | loop fusion | flops 19922944 | bytes 4204544 | tf_op jit(solution)/shard_map/convert.28
  107.2 9.9 %while.40 = (s32[]{:T(128)}, f32[4,256,4]{1,0,2:T(4,128)S(1)}, s32[2,2,1024]{2,1,0:T(2,128)S(1)}, s32[4]{0:T(128)S(1)}, f32[2,2,1024]{2,1,0:T(2,128)S(1)}, /*ind...) while((s32[]{:T(128)}, f32[4,256,4]{1,0,2:T(4,128)S(1)}, ...), condition=%wide.region_3.4_spmd, body=%wide.region_0.3_spmd.sunk | while | flops 35309604 | bytes 668095 | solution.py:213
  117.3 24.2 %all_to_all.55 = f32[16,1,256]{2,1,0:T(1,128)S(1)} all-to-all(f32[16,1,256]{2,1,0:T(1,128)S(1)} %reshape.1732), channel_id=1, replica_groups=mesh['cuts'=32,'tr'=16] {'tr'}, dimensions={0} | all-to-all | bytes 32768 | tf_op jit(solution)/shard_map/all_to_all | solution.py:42
  143.5 15.0 %all_to_all.56 = f32[16,1,256]{2,1,0:T(1,128)S(1)} all-to-all(f32[16,1,256]{2,1,0:T(1,128)S(1)} %reshape.1734), channel_id=1, replica_groups=mesh['cuts'=32,'tr'=16] {'tr'}, dimensions={0} | all-to-all | bytes 32768 | tf_op jit(solution)/shard_map/all_to_all | solution.py:54
  167.8 4.6 %collective-permute-start.3 = (bf16[512,512]{1,0:T(8,128)(2,1)S(1)}, bf16[512,512]{1,0:T(8,128)(2,1)}, u32[]{:S(2)}, u32[]{:S(2)}) collective-permute-start(bf16[512,512]{1,0:T(8,128)(2,1)S(1)} %fusion.109), channel_id=1, source_target_pairs={{0,480},{16,496},{32,0},{48,16},{64,32},{80,48},{96,64},{112,80},{... | collective-permute-start | bytes 1572872 | tf_op jit(solution)/shard_map/ppermute | solution.py:31
  189.3 16.2 %all_to_all.57 = bf16[16,32,128]{2,1,0:T(8,128)(2,1)S(1)} all-to-all(bf16[16,32,128]{2,1,0:T(8,128)(2,1)S(1)} %constant_dynamic-update-slice_fusion.16), channel_id=1, replica_groups=mesh['cuts'=32,'tr'=16] {'tr'}, dimensions={0} | all-to-all | bytes 262144 | tf_op jit(solution)/shard_map/all_to_all | solution.py:165
  218.5 9.9 %while.41 = (s32[]{:T(128)}, f32[4,256,4]{1,0,2:T(4,128)S(1)}, s32[2,2,1024]{2,1,0:T(2,128)S(1)}, s32[4]{0:T(128)S(1)}, f32[2,2,1024]{2,1,0:T(2,128)S(1)}, /*ind...) while((s32[]{:T(128)}, f32[4,256,4]{1,0,2:T(4,128)S(1)}, ...), condition=%wide.region_8.9_spmd, body=%wide.region_5.8_spmd.sunk | while | flops 35309604 | bytes 668095 | solution.py:213
  228.6 18.5 %all_to_all.58 = f32[16,1,256]{2,1,0:T(1,128)S(1)} all-to-all(f32[16,1,256]{2,1,0:T(1,128)S(1)} %reshape.1736), channel_id=1, replica_groups=mesh['cuts'=32,'tr'=16] {'tr'}, dimensions={0} | all-to-all | bytes 32768 | tf_op jit(solution)/shard_map/all_to_all | solution.py:42
  248.0 15.0 %all_to_all.59 = f32[16,1,256]{2,1,0:T(1,128)S(1)} all-to-all(f32[16,1,256]{2,1,0:T(1,128)S(1)} %reshape.1738), channel_id=1, replica_groups=mesh['cuts'=32,'tr'=16] {'tr'}, dimensions={0} | all-to-all | bytes 32768 | tf_op jit(solution)/shard_map/all_to_all | solution.py:54
  266.4 4.8 %collective-permute-start.6 = (bf16[512,512]{1,0:T(8,128)(2,1)S(1)}, bf16[512,512]{1,0:T(8,128)(2,1)}, u32[]{:S(2)}, u32[]{:S(2)}) collective-permute-start(bf16[512,512]{1,0:T(8,128)(2,1)S(1)} %fusion.110), channel_id=1, source_target_pairs={{0,64},{16,80},{32,96},{48,112},{64,128},{80,144},{96,160},{112,17... | collective-permute-start | bytes 1572872 | tf_op jit(solution)/shard_map/ppermute | solution.py:31
  279.9 6.4 %collective-permute-done.7 = bf16[512,512]{1,0:T(8,128)(2,1)} collective-permute-done((bf16[512,512]{1,0:T(8,128)(2,1)S(1)}, bf16[512,512]{1,0:T(8,128)(2,1)}, u32[]{:S(2)}, u32[]{:S(2)}) %collective-permute-start.7) | collective-permute-done | bytes 524320 | tf_op jit(solution)/shard_map/ppermute | solution.py:31
  296.0 15.7 %all_to_all.60 = bf16[16,32,128]{2,1,0:T(8,128)(2,1)S(1)} all-to-all(bf16[16,32,128]{2,1,0:T(8,128)(2,1)S(1)} %constant_dynamic-update-slice_fusion.32), channel_id=1, replica_groups=mesh['cuts'=32,'tr'=16] {'tr'}, dimensions={0} | all-to-all | bytes 262144 | tf_op jit(solution)/shard_map/all_to_all | solution.py:165
  324.7 9.9 %while.42 = (s32[]{:T(128)}, f32[4,256,4]{1,0,2:T(4,128)S(1)}, s32[2,2,1024]{2,1,0:T(2,128)S(1)}, s32[4]{0:T(128)S(1)}, f32[2,2,1024]{2,1,0:T(2,128)S(1)}, /*ind...) while((s32[]{:T(128)}, f32[4,256,4]{1,0,2:T(4,128)S(1)}, ...), condition=%wide.region_13.14_spmd, body=%wide.region_10.13_spmd.sunk | while | flops 35309604 | bytes 668095 | solution.py:213
  334.8 18.7 %all_to_all.61 = f32[16,1,256]{2,1,0:T(1,128)S(1)} all-to-all(f32[16,1,256]{2,1,0:T(1,128)S(1)} %reshape.1740), channel_id=1, replica_groups=mesh['cuts'=32,'tr'=16] {'tr'}, dimensions={0} | all-to-all | bytes 32768 | tf_op jit(solution)/shard_map/all_to_all | solution.py:42
  354.3 15.0 %all_to_all.62 = f32[16,1,256]{2,1,0:T(1,128)S(1)} all-to-all(f32[16,1,256]{2,1,0:T(1,128)S(1)} %reshape.1742), channel_id=1, replica_groups=mesh['cuts'=32,'tr'=16] {'tr'}, dimensions={0} | all-to-all | bytes 32768 | tf_op jit(solution)/shard_map/all_to_all | solution.py:54
  372.7 6.0 %collective-permute-start.10 = (bf16[512,512]{1,0:T(8,128)(2,1)S(1)}, bf16[512,512]{1,0:T(8,128)(2,1)S(1)}, u32[]{:S(2)}, u32[]{:S(2)}) collective-permute-start(bf16[512,512]{1,0:T(8,128)(2,1)S(1)} %fusion.112), channel_id=1, source_target_pairs={{0,96},{16,112},{32,128},{48,144},{64,160},{80,176},{96,192},{112,... | collective-permute-start | bytes 1572872 | tf_op jit(solution)/shard_map/ppermute | solution.py:31
  385.4 8.2 %collective-permute-done.11 = bf16[512,512]{1,0:T(8,128)(2,1)} collective-permute-done((bf16[512,512]{1,0:T(8,128)(2,1)S(1)}, bf16[512,512]{1,0:T(8,128)(2,1)}, u32[]{:S(2)}, u32[]{:S(2)}) %collective-permute-start.11) | collective-permute-done | bytes 524320 | tf_op jit(solution)/shard_map/ppermute | solution.py:31
  401.0 15.7 %all_to_all.63 = bf16[16,32,128]{2,1,0:T(8,128)(2,1)S(1)} all-to-all(bf16[16,32,128]{2,1,0:T(8,128)(2,1)S(1)} %constant_dynamic-update-slice_fusion.48), channel_id=1, replica_groups=mesh['cuts'=32,'tr'=16] {'tr'}, dimensions={0} | all-to-all | bytes 262144 | tf_op jit(solution)/shard_map/all_to_all | solution.py:165
  429.0 9.5 %while.43 = (s32[]{:T(128)}, f32[4,256,4]{1,0,2:T(4,128)S(1)}, s32[2,2,1024]{2,1,0:T(2,128)S(1)}, s32[4]{0:T(128)S(1)}, f32[2,2,1024]{2,1,0:T(2,128)S(1)}, /*ind...) while((s32[]{:T(128)}, f32[4,256,4]{1,0,2:T(4,128)S(1)}, ...), condition=%wide.region_18.19_spmd, body=%wide.region_15.18_spmd.sunk | while | flops 35309604 | bytes 668095 | solution.py:213
  438.7 18.7 %all_to_all.64 = f32[16,1,256]{2,1,0:T(1,128)S(1)} all-to-all(f32[16,1,256]{2,1,0:T(1,128)S(1)} %reshape.1744), channel_id=1, replica_groups=mesh['cuts'=32,'tr'=16] {'tr'}, dimensions={0} | all-to-all | bytes 32768 | tf_op jit(solution)/shard_map/all_to_all | solution.py:42
  (808 shorter events, 171.9 us)
Async XLA Ops:
  8.5 17.8 %copy-start.5 = (s32[2,1,2,1024]{3,2,1,0:T(2,128)S(1)}, s32[2,1,2,1024]{3,2,1,0:T(2,128)}, u32[]{:S(2)}) copy-start(s32[2,1,2,1024]{3,2,1,0:T(2,128)} %param.13) | copy-start | bytes 49156
  8.5 17.8 %copy-start.6 = (f32[2,1,2,1024]{3,2,1,0:T(2,128)S(1)}, f32[2,1,2,1024]{3,2,1,0:T(2,128)}, u32[]{:S(2)}) copy-start(f32[2,1,2,1024]{3,2,1,0:T(2,128)} %param.14) | copy-start | bytes 49156
  8.6 17.9 %copy-start.10 = (f32[2,1,1024]{2,1,0:T(1,128)S(1)}, f32[2,1,1024]{2,1,0:T(1,128)}, u32[]{:S(2)}) copy-start(f32[2,1,1024]{2,1,0:T(1,128)} %param.15) | copy-start | bytes 24580
  59.3 34.0 %all-to-all-start = ((bf16[16,32,128]{2,1,0:T(8,128)(2,1)}), bf16[16,32,128]{2,1,0:T(8,128)(2,1)S(1)}, u32[]{:S(2)}, u32[]{:S(2)}) async-start(bf16[16,32,128]{2,1,0:T(8,128)(2,1)} %constant_dynamic-update-slice_fusion), calls=%async_computation | async-start | bytes 262144 | tf_op jit(solution)/shard_map/all_to_all | solution.py:165
  97.3 5.2 %collective-permute-start = (bf16[1,2,512]{2,1,0:T(2,128)(2,1)S(1)}, bf16[1,2,512]{2,1,0:T(2,128)(2,1)S(1)}, u32[]{:S(2)}, u32[]{:S(2)}) collective-permute-start(bf16[1,2,512]{2,1,0:T(2,128)(2,1)S(1)} %get-tuple-element.402), channel_id=1, source_target_pairs={{0,1},{1,2},{2,3},{3,4},{4,5},{5,6},{6,7},{7,8},{8,9},{9,10},{10,1... | collective-permute-start | bytes 6152 | tf_op jit(solution)/shard_map/ppermute | solution.py:19
  101.2 5.5 %collective-permute-start.1 = (bf16[1,2,512]{2,1,0:T(2,128)(2,1)S(1)}, bf16[1,2,512]{2,1,0:T(2,128)(2,1)S(1)}, u32[]{:S(2)}, u32[]{:S(2)}) collective-permute-start(bf16[1,2,512]{2,1,0:T(2,128)(2,1)S(1)} %get-tuple-element.403), channel_id=1, source_target_pairs={{1,0},{2,1},{3,2},{4,3},{5,4},{6,5},{7,6},{8,7},{9,8},{10,9},{11,1... | collective-permute-start | bytes 6152 | tf_op jit(solution)/shard_map/ppermute | solution.py:21
  107.1 35.6 %copy-start.11 = (f32[2,1,2,64]{3,2,1,0:T(2,128)S(1)}, f32[2,1,2,64]{3,2,1,0:T(2,128)}, u32[]{:S(2)}) copy-start(f32[2,1,2,64]{3,2,1,0:T(2,128)} %param.16) | copy-start | bytes 3076
  107.2 52.3 %copy-start.24 = (f32[1,1,512]{2,1,0:T(1,128)S(1)}, f32[1,1,512]{2,1,0:T(1,128)}, u32[]{:S(2)}) copy-start(f32[1,1,512]{2,1,0:T(1,128)} %copy-done.23) | copy-start | bytes 6148
  161.8 13.3 %collective-permute-start.2 = (bf16[512,512]{1,0:T(8,128)(2,1)S(1)}, bf16[512,512]{1,0:T(8,128)(2,1)}, u32[]{:S(2)}, u32[]{:S(2)}) collective-permute-start(bf16[512,512]{1,0:T(8,128)(2,1)S(1)} %fusion.108), channel_id=1, source_target_pairs={{0,32},{16,48},{32,64},{48,80},{64,96},{80,112},{96,128},{112,144}... | collective-permute-start | bytes 1572872 | tf_op jit(solution)/shard_map/ppermute | solution.py:31
  167.8 11.3 %collective-permute-start.3 = (bf16[512,512]{1,0:T(8,128)(2,1)S(1)}, bf16[512,512]{1,0:T(8,128)(2,1)}, u32[]{:S(2)}, u32[]{:S(2)}) collective-permute-start(bf16[512,512]{1,0:T(8,128)(2,1)S(1)} %fusion.109), channel_id=1, source_target_pairs={{0,480},{16,496},{32,0},{48,16},{64,32},{80,48},{96,64},{112,80},{... | collective-permute-start | bytes 1572872 | tf_op jit(solution)/shard_map/ppermute | solution.py:31
  209.5 4.3 collective-permute-start.4
  212.5 5.5 %collective-permute-start.5 = (bf16[1,2,512]{2,1,0:T(2,128)(2,1)S(1)}, bf16[1,2,512]{2,1,0:T(2,128)(2,1)S(1)}, u32[]{:S(2)}, u32[]{:S(2)}) collective-permute-start(bf16[1,2,512]{2,1,0:T(2,128)(2,1)S(1)} %get-tuple-element.401), channel_id=1, source_target_pairs={{1,0},{2,1},{3,2},{4,3},{5,4},{6,5},{7,6},{8,7},{9,8},{10,9},{11,1... | collective-permute-start | bytes 6152 | tf_op jit(solution)/shard_map/ppermute | solution.py:21
  218.4 29.4 %copy-start.9 = (f32[2,1,2,64]{3,2,1,0:T(2,128)S(1)}, f32[2,1,2,64]{3,2,1,0:T(2,128)}, u32[]{:S(2)}) copy-start(f32[2,1,2,64]{3,2,1,0:T(2,128)} %copy-done.8) | copy-start | bytes 3076
  218.4 45.5 %copy-start.25 = (f32[1,1,512]{2,1,0:T(1,128)S(1)}, f32[1,1,512]{2,1,0:T(1,128)}, u32[]{:S(2)}) copy-start(f32[1,1,512]{2,1,0:T(1,128)} %copy-done.23) | copy-start | bytes 6148
  266.4 13.6 %collective-permute-start.6 = (bf16[512,512]{1,0:T(8,128)(2,1)S(1)}, bf16[512,512]{1,0:T(8,128)(2,1)}, u32[]{:S(2)}, u32[]{:S(2)}) collective-permute-start(bf16[512,512]{1,0:T(8,128)(2,1)S(1)} %fusion.110), channel_id=1, source_target_pairs={{0,64},{16,80},{32,96},{48,112},{64,128},{80,144},{96,160},{112,17... | collective-permute-start | bytes 1572872 | tf_op jit(solution)/shard_map/ppermute | solution.py:31
  273.7 12.7 %collective-permute-start.7 = (bf16[512,512]{1,0:T(8,128)(2,1)S(1)}, bf16[512,512]{1,0:T(8,128)(2,1)}, u32[]{:S(2)}, u32[]{:S(2)}) collective-permute-start(bf16[512,512]{1,0:T(8,128)(2,1)S(1)} %fusion.111), channel_id=1, source_target_pairs={{0,448},{16,464},{32,480},{48,496},{64,0},{80,16},{96,32},{112,48}... | collective-permute-start | bytes 1572872 | tf_op jit(solution)/shard_map/ppermute | solution.py:31
  315.8 4.5 collective-permute-start.8
  318.8 5.5 %collective-permute-start.9 = (bf16[1,2,512]{2,1,0:T(2,128)(2,1)S(1)}, bf16[1,2,512]{2,1,0:T(2,128)(2,1)S(1)}, u32[]{:S(2)}, u32[]{:S(2)}) collective-permute-start(bf16[1,2,512]{2,1,0:T(2,128)(2,1)S(1)} %get-tuple-element.399), channel_id=1, source_target_pairs={{1,0},{2,1},{3,2},{4,3},{5,4},{6,5},{7,6},{8,7},{9,8},{10,9},{11,1... | collective-permute-start | bytes 6152 | tf_op jit(solution)/shard_map/ppermute | solution.py:21
  324.7 45.6 %copy-start.26 = (f32[1,1,512]{2,1,0:T(1,128)S(1)}, f32[1,1,512]{2,1,0:T(1,128)}, u32[]{:S(2)}) copy-start(f32[1,1,512]{2,1,0:T(1,128)} %copy-done.23) | copy-start | bytes 6148
  372.7 12.7 %collective-permute-start.10 = (bf16[512,512]{1,0:T(8,128)(2,1)S(1)}, bf16[512,512]{1,0:T(8,128)(2,1)S(1)}, u32[]{:S(2)}, u32[]{:S(2)}) collective-permute-start(bf16[512,512]{1,0:T(8,128)(2,1)S(1)} %fusion.112), channel_id=1, source_target_pairs={{0,96},{16,112},{32,128},{48,144},{64,160},{80,176},{96,192},{112,... | collective-permute-start | bytes 1572872 | tf_op jit(solution)/shard_map/ppermute | solution.py:31
  381.2 12.4 %collective-permute-start.11 = (bf16[512,512]{1,0:T(8,128)(2,1)S(1)}, bf16[512,512]{1,0:T(8,128)(2,1)}, u32[]{:S(2)}, u32[]{:S(2)}) collective-permute-start(bf16[512,512]{1,0:T(8,128)(2,1)S(1)} %fusion.113), channel_id=1, source_target_pairs={{0,416},{16,432},{32,448},{48,464},{64,480},{80,496},{96,0},{112,1... | collective-permute-start | bytes 1572872 | tf_op jit(solution)/shard_map/ppermute | solution.py:31
  399.0 17.7 %copy-start.4 = (bf16[512,2048]{1,0:T(8,128)(2,1)S(1)}, bf16[512,2048]{1,0:T(8,128)(2,1)}, u32[]{:S(2)}) copy-start(bf16[512,2048]{1,0:T(8,128)(2,1)} %get-tuple-element.420) | copy-start | bytes 6291460
  420.1 4.3 collective-permute-start.12
  423.1 5.5 %collective-permute-start.13 = (bf16[1,2,512]{2,1,0:T(2,128)(2,1)S(1)}, bf16[1,2,512]{2,1,0:T(2,128)(2,1)S(1)}, u32[]{:S(2)}, u32[]{:S(2)}) collective-permute-start(bf16[1,2,512]{2,1,0:T(2,128)(2,1)S(1)} %get-tuple-element.397), channel_id=1, source_target_pairs={{1,0},{2,1},{3,2},{4,3},{5,4},{6,5},{7,6},{8,7},{9,8},{10,9},{11,1... | collective-permute-start | bytes 6152 | tf_op jit(solution)/shard_map/ppermute | solution.py:21
  (18 other events, 130.8 us)
